TPU v7x, 32 devices: a whole 2x2x4 slice. The times are simulated.
32 devices in a mesh: grp: 8 (over y, x, core), dom: 4 (over z).
Axes of the slice: x: 2, y: 2, z: 4, core: 2. Of those that a mesh axis runs over, the one named last changes fastest.
Arguments:
- surplus: float32 [128, 512, 512], P('grp', 'dom'), may hold values from -0.4 to 0.4
- block_ids: int32 [128, 512], P('grp', 'dom'), may hold values from 0 to 4095, as said below
- coef: int32 [128], P('grp'), may hold values from -4 to 6, as said below
Outputs:
- updated: float32 [128, 512, 512], P('grp', 'dom')
Inputs may be any that keep to these rules, and one draw needn't show every extreme that they name: `block_ids`: for each grid, the slots in columns d * 128 to (d + 1) * 128 - 1 hold 128 different numbers from d * 1024 to (d + 1) * 1024 - 1. `coef`: each coefficient is one of 1, -4, 6.
All inputs are finite; a program needn't handle non-finite values.
Results may differ from a plain program's by a relative error of at most 0.000071.
Values sent between devices are 32-bit elements; how exact they have to be, the bound alone decides.
A program may use at most 64 MiB of HBM per device.

v0:
```python
import jax
import jax.numpy as jnp
from jax import lax
from jax.sharding import PartitionSpec as P

NBD = 1024


def local(surplus, block_ids, coef):
    offset = lax.axis_index("dom") * NBD
    local_ids = block_ids - offset
    columns = lax.broadcasted_iota(jnp.int32, (1, 1, NBD), 2)
    onehot = (local_ids[:, :, None] == columns).astype(jnp.float32)
    scaled = surplus * coef.astype(jnp.float32)[:, None, None]
    partial_sum = jnp.einsum("gkn,gkb->nb", onehot, scaled, precision=lax.Precision.HIGHEST)
    combined = lax.psum(partial_sum, "grp")
    return jnp.einsum("gkn,nb->gkb", onehot, combined, precision=lax.Precision.HIGHEST)


def solution(mesh):
    return jax.shard_map(
        local,
        mesh=mesh,
        in_specs=(P("grp", "dom", None), P("grp", "dom"), P("grp")),
        out_specs=P("grp", "dom", None),
        check_vma=False,
    )
```

profile of v0, /device:TPU:0, one launch (start us, length us, event | category | flops | bytes accessed | tf_op | source)
XLA Modules:
  0.0 106.6 jit_solution(6642148042508687133)
XLA Ops:
  6.5 0.0 all-reduce.2.cloned.1.call-start
  6.5 0.7 convert_element_type.4
  7.2 0.7 broadcast_subtract_fusion
  7.9 16.8 %fusion.7 = f32[1024,512]{1,0:T(8,128)} fusion(f32[16,128,512]{2,1,0:T(8,128)} %param.3, f32[16]{0:T(128)S(1)} %convert_element_type.4, s32[16,128]{1,0:T(8,128)S(1)} %broadcast_subtract_fusion), kind=kOutput, calls=%fused_computation.8 | convolution fusion | flops 12888047616 | bytes 6299712 | tf_op jit(solution)/shard_map/gkn,gkb->nb/dot_general | solution.py:15
  24.7 0.0 all-reduce.2.cloned.1.call-update
  24.7 64.6 %all-reduce.2.cloned.1.call-done = f32[1024,512]{1,0:T(8,128)} async-done(((f32[1024,512]{1,0:T(8,128)}), f32[1024,512]{1,0:T(8,128)}) %all-reduce.2.cloned.1.call-update) | async-done | bytes 2097168 | tf_op jit(solution)/shard_map/psum | solution.py:16
  89.3 10.4 %fusion = f32[16,128,512]{2,1,0:T(8,128)} fusion(s32[16,128]{1,0:T(8,128)S(1)} %broadcast_subtract_fusion, f32[1024,512]{1,0:T(8,128)} %all-reduce.2.cloned.1.call-done), kind=kOutput, calls=%fused_computation.1 | convolution fusion | flops 12886999040 | bytes 6299648 | tf_op jit(solution)/shard_map/gkn,nb->gkb/dot_general | solution.py:17
Async XLA Ops:
  6.5 82.8 %all-reduce.2.cloned.1.call-start = ((), (), s32[]{:S(2)}) async-start(), calls=%async_computation | async-start | bytes 4194304 | tf_op jit(solution)/shard_map/psum | solution.py:16
Sparse Core Ops, SparseCore 0:
  24.8 64.4 all-reduce.1
where the time goes:
time: 107 us
  waiting for transfers between devices  64.7 us (60%)
  matrix products  27.2 us (25%)
  between operations  13.4 us (13%)
  other arithmetic  1.36 us (1%)
    psum x1, waiting for transfers between devices, local(): combined = lax.psum(partial_sum, 'grp')  64.6 us
    dot_general x1, matrix products, local(): jnp.einsum('gkn,gkb->nb', onehot, scaled, precision=lax.Precision.HIGHEST)  16.8 us
    dot_general x1, matrix products, local(): jnp.einsum('gkn,nb->gkb', onehot, combined, precision=lax.Precision.HIGHEST)  10.4 us
  transfers between devices with their start and end apart: 1, of which 1 were waited for; matrix products, arithmetic and copies ran while one was open for 0% of the time, Pallas kernels for 0%

commit v1 on v0

--- a/solution.py
+++ b/solution.py
@@ -13,7 +13,7 @@
     onehot = (local_ids[:, :, None] == columns).astype(jnp.float32)
     scaled = surplus * coef.astype(jnp.float32)[:, None, None]
     partial_sum = jnp.einsum("gkn,gkb->nb", onehot, scaled, precision=lax.Precision.HIGHEST)
-    combined = lax.psum(partial_sum, "grp")
+    combined = jnp.sum(lax.all_gather(partial_sum, "grp"), axis=0)
     return jnp.einsum("gkn,nb->gkb", onehot, combined, precision=lax.Precision.HIGHEST)
 
 

time: 107 us -> 141 us (1.32)
  waiting for transfers between devices: 64.7 us -> 92.6 us
  other arithmetic: 1.36 us -> 9.53 us
  matrix products: 27.2 us -> 25.3 us
    all_gather x0 -> x1, waiting for transfers between devices: none -> 92.6 us  [local(): combined = jnp.sum(lax.all_gather(partial_sum, 'grp'), axis=0)]
    psum x1 -> x0, waiting for transfers between devices: 64.6 us -> none  [local(): combined = lax.psum(partial_sum, 'grp')]
    reduce_sum x0 -> x1, other arithmetic: none -> 8.17 us  [local(): combined = jnp.sum(lax.all_gather(partial_sum, 'grp'), axis=0)]
    dot_general x1, matrix products: 10.4 us -> 8.55 us  [local(): jnp.einsum('gkn,nb->gkb', onehot, combined, precision=lax.Precision.HIGHEST)]
where the time goes in v1:
time: 141 us
  waiting for transfers between devices  92.6 us (66%)
  matrix products  25.3 us (18%)
  between operations  13.4 us (10%)
  other arithmetic  9.53 us (7%)
    all_gather x1, waiting for transfers between devices, local(): combined = jnp.sum(lax.all_gather(partial_sum, 'grp'), axis=0)  92.6 us
    dot_general x1, matrix products, local(): jnp.einsum('gkn,gkb->nb', onehot, scaled, precision=lax.Precision.HIGHEST)  16.8 us
    dot_general x1, matrix products, local(): jnp.einsum('gkn,nb->gkb', onehot, combined, precision=lax.Precision.HIGHEST)  8.55 us
    reduce_sum x1, other arithmetic, local(): combined = jnp.sum(lax.all_gather(partial_sum, 'grp'), axis=0)  8.17 us
  transfers between devices with their start and end apart: 1, of which 1 were waited for; matrix products, arithmetic and copies ran while one was open for 0% of the time, Pallas kernels for 0%

profile of v1, /device:TPU:0, one launch (start us, length us, event | category | flops | bytes accessed | tf_op | source)
XLA Modules:
  0.0 140.9 jit_solution(7884906933654413628)
XLA Ops:
  6.5 0.0 all-gather.3.cloned.1.call-start
  6.5 0.7 convert_element_type.4
  7.2 0.7 broadcast_subtract_fusion
  7.9 16.8 %fusion.7 = f32[1024,512]{1,0:T(8,128)} fusion(f32[16,128,512]{2,1,0:T(8,128)} %param.3, f32[16]{0:T(128)S(1)} %convert_element_type.4, s32[16,128]{1,0:T(8,128)S(1)} %broadcast_subtract_fusion), kind=kOutput, calls=%fused_computation.8 | convolution fusion | flops 12888047616 | bytes 6299712 | tf_op jit(solution)/shard_map/gkn,gkb->nb/dot_general | solution.py:15
  24.7 0.0 all-gather.3.cloned.1.call-update
  24.7 92.6 %all-gather.3.cloned.1.call-done = f32[8192,512]{1,0:T(8,128)} async-done(((f32[1024,512]{1,0:T(8,128)}), f32[8192,512]{1,0:T(8,128)}) %all-gather.3.cloned.1.call-update) | async-done | bytes 16777232 | tf_op jit(solution)/shard_map/all_gather | solution.py:16
  117.3 8.2 %reduce_sum.9 = f32[1024,512]{1,0:T(8,128)S(1)} reduce(f32[8,1024,512]{2,1,0:T(8,128)} %bitcast.6, f32[]{:T(128)} %constant.2.clone.1), dimensions={0}, to_apply=%region_0.0 | reduce | flops 3670016 | bytes 18874372 | tf_op jit(solution)/shard_map/reduce_sum | solution.py:16
  125.5 8.6 %fusion = f32[16,128,512]{2,1,0:T(8,128)} fusion(s32[16,128]{1,0:T(8,128)S(1)} %broadcast_subtract_fusion, f32[1024,512]{1,0:T(8,128)S(1)} %reduce_sum.9), kind=kOutput, calls=%fused_computation.1 | convolution fusion | flops 12886999040 | bytes 6299648 | tf_op jit(solution)/shard_map/gkn,nb->gkb/dot_general | solution.py:17
Async XLA Ops:
  6.5 110.8 %all-gather.3.cloned.1.call-start = ((), (), s32[]{:S(2)}) async-start(), calls=%async_computation | async-start | bytes 18874368 | tf_op jit(solution)/shard_map/all_gather | solution.py:16
Sparse Core Ops, SparseCore 0:
  24.8 92.4 all-gather.2
